TPU v7x, 256 devices: a 8x8x2 block of a 8x8x16 slice. The times are simulated.
256 devices in a mesh: rep: 2 (over z), tp: 16 (over y, core), sub: 8 (over x).
Axes of the slice: x: 8, y: 8, z: 2, core: 2. Of those that a mesh axis runs over, the one named last changes fastest.
The devices are a block of a 8x8x16 slice.
Arguments:
- acts: bfloat16 [2048, 16384], P(('rep', 'tp'), 'sub'), parts along dimension 0, may hold values from -6 to 6
- q_src: bfloat16 [32768, 16384], P(('rep', 'sub'), 'tp'), parts along dimension 0, may hold values from -0.046875 to 0.046875
- kv_src: bfloat16 [32768, 2048], P(('rep', 'sub'), 'tp'), parts along dimension 0, may hold values from -0.046875 to 0.046875
- q_src_heads: int32 [128], replicated, may hold values from 0 to 127, as said below
- q_tgt_heads: int32 [128], replicated, may hold values from 0 to 127, as said below
- kv_tgt_heads: int32 [16], replicated, may hold values from 0 to 7, as said below
Outputs:
- q_new: bfloat16 [32768, 16384], P(('rep', 'sub'), 'tp'), parts along dimension 0
- kv_new: bfloat16 [32768, 4096], P(('rep', 'sub'), 'tp'), parts along dimension 0
- qkv: bfloat16 [2048, 20480], P(('rep', 'sub'), 'tp'), parts along dimension 0
There are 2 independent parts, one for each index of `rep`. A program takes and returns all parts, laid end to end along the dimension named above; an argument that names none is the same for every part. Nothing has to cross between parts.
Inputs may be any that keep to these rules, and one draw needn't show every extreme that they name: q_src_heads and q_tgt_heads are permutations. Source block t is entries t * 8 to (t + 1) * 8 - 1 of q_src_heads, target block j the same entries of q_tgt_heads. With s = 4, source block t shares exactly 2 heads with target block (t + min(1, s - 1)) mod 16 and with each target block (t + k * s) mod 16 for k from 1 to 3, and none with any other. `q_tgt_heads`: see q_src_heads. `kv_tgt_heads`: every key-value head appears exactly twice.
All inputs are finite; a program needn't handle non-finite values.
Results may differ from a plain program's by a relative error of at most 0.001.
Values may be sent and summed in bfloat16 or wider, within the bound.
A program may use at most 128 MiB of HBM per device.

v0:
```python
import jax
import jax.numpy as jnp
from jax import lax
from jax.sharding import PartitionSpec as P

HD = 128


def from_behind(block, axis, distance):
    devices = range(lax.axis_size(axis))
    route = [((i - distance) % len(devices), i) for i in devices]
    return lax.ppermute(block, axis, route)


def per_device(acts, q_src, kv_src, q_src_heads, q_tgt_heads, kv_tgt_heads):
    tp_count = lax.axis_size("tp")
    my_index = lax.axis_index("tp")
    row_count = q_src.shape[0]
    q_local = q_src.shape[1] // HD
    capacity = max(2, q_local // tp_count)
    select_count = q_local // capacity
    stride = tp_count // select_count
    head_count = q_src_heads.shape[0]
    head_ids = jnp.arange(head_count, dtype=jnp.int32)
    matches = (q_src_heads[None, :] == q_tgt_heads[:, None]).astype(jnp.int32)
    target_pos = jnp.sum(matches * head_ids[:, None], axis=0)
    slot_of = jnp.sum(matches * head_ids[None, :], axis=1)
    target_dev = target_pos // q_local
    source_dev = head_ids // q_local
    earlier = (
        (source_dev[:, None] == source_dev[None, :])
        & (target_dev[:, None] == target_dev[None, :])
        & (head_ids[None, :] < head_ids[:, None])
    )
    slot_rank = jnp.sum(earlier.astype(jnp.int32), axis=1)
    own_target = lax.dynamic_slice_in_dim(target_dev, my_index * q_local, q_local)
    own_rank = lax.dynamic_slice_in_dim(slot_rank, my_index * q_local, q_local)
    buffer_ids = jnp.arange(tp_count * capacity, dtype=jnp.int32)
    slot_hit = ((own_target * capacity + own_rank)[None, :] == buffer_ids[:, None]).astype(
        jnp.int32
    )
    pick_slot = jnp.sum(slot_hit * jnp.arange(q_local, dtype=jnp.int32)[None, :], axis=1)
    my_slots = lax.dynamic_slice_in_dim(slot_of, my_index * q_local, q_local)
    pick_table = pick_slot.reshape(tp_count, capacity)
    q_three = q_src.reshape(row_count, q_local, HD)
    pieces = []
    for step_number in range(select_count):
        if step_number == 0:
            distance = min(1, stride - 1)
        else:
            distance = step_number * stride
        target_block = (my_index + distance) % tp_count
        chosen_slots = lax.dynamic_index_in_dim(pick_table, target_block, 0, keepdims=False)
        outgoing_piece = jnp.take(q_three, chosen_slots, axis=1)
        outgoing_piece = from_behind(outgoing_piece, "tp", distance)
        pieces.append(outgoing_piece)
    stacked = jnp.concatenate(pieces, axis=1)
    source_block = my_slots // q_local
    offset = (my_index - source_block) % tp_count
    shift_rank = jnp.where(offset % stride == 0, offset // stride, 0)
    compact_ids = shift_rank * capacity + slot_rank[my_slots]
    q_new = jnp.take(stacked, compact_ids, axis=1).reshape(row_count, q_local * HD)
    kv_slots = kv_tgt_heads.shape[0] // tp_count
    kv_whole = lax.all_gather(kv_src, "tp", axis=1, tiled=True)
    own_kv = lax.dynamic_slice_in_dim(kv_tgt_heads, my_index * kv_slots, kv_slots)
    kv_three = kv_whole.reshape(row_count, kv_whole.shape[1] // (2 * HD), 2 * HD)
    kv_new = jnp.take(kv_three, own_kv, axis=1).reshape(row_count, kv_slots * 2 * HD)
    gathered = lax.all_gather(acts, "tp", axis=0, tiled=True)
    joined_cols = jnp.concatenate([q_new, kv_new], axis=1)
    qkv = lax.psum_scatter(
        jnp.dot(gathered, joined_cols, preferred_element_type=jnp.float32),
        "sub",
        scatter_dimension=0,
        tiled=True,
    ).astype(jnp.bfloat16)
    return (q_new, kv_new, qkv)


def solution(mesh):
    in_specs = (
        P(("rep", "tp"), "sub"),
        P(("rep", "sub"), "tp"),
        P(("rep", "sub"), "tp"),
        P(),
        P(),
        P(),
    )
    out_specs = (P(("rep", "sub"), "tp"), P(("rep", "sub"), "tp"), P(("rep", "sub"), "tp"))
    return jax.shard_map(
        per_device, mesh=mesh, in_specs=in_specs, out_specs=out_specs, check_vma=False
    )
```

profile of v0, /device:TPU:513, one launch (start us, length us, event | category | flops | bytes accessed | tf_op | source)
XLA Modules:
  0.0 309.0 jit_solution(1556637233331579625)
XLA Ops:
  7.2 2.0 copy.30
  11.6 6.4 %copy.24 = bf16[2048,1024]{0,1:T(8,128)(2,1)} copy(bf16[2048,1024]{1,0:T(8,128)(2,1)} %param.9) | data formatting | bytes 8388608 | tf_op args[1]
  18.0 6.5 %copy.25 = bf16[2048,8,128]{2,0,1:T(8,128)(2,1)} copy(bf16[2048,8,128]{0,2,1:T(8,128)(2,1)} %bitcast.43) | data formatting | bytes 8388608 | tf_op jit(solution)/shard_map/reshape | solution.py:45
  24.5 2.9 gather_fusion.2
  27.6 3.9 %collective-permute-start = (bf16[2048,2,128]{2,0,1:T(8,128)(2,1)S(1)}, bf16[2048,2,128]{2,0,1:T(8,128)(2,1)}, u32[]{:S(2)}, u32[]{:S(2)}) collective-permute-start(bf16[2048,2,128]{2,0,1:T(8,128)(2,1)S(1)} %select_bitcast_fusion.3), channel_id=1, source_target_pairs={{120,0},{0,8},{8,16},{16,24},{24,32},{32,40},{40,48},{48,56},{56,6... | collective-permute-start | bytes 3145736 | tf_op jit(solution)/shard_map/ppermute | solution.py:12
  31.5 2.9 gather_fusion.3
  34.6 4.8 %collective-permute-start.1 = (bf16[2048,2,128]{2,0,1:T(8,128)(2,1)S(1)}, bf16[2048,2,128]{2,0,1:T(8,128)(2,1)}, u32[]{:S(2)}, u32[]{:S(2)}) collective-permute-start(bf16[2048,2,128]{2,0,1:T(8,128)(2,1)S(1)} %select_bitcast_fusion.2), channel_id=1, source_target_pairs={{96,0},{104,8},{112,16},{120,24},{0,32},{8,40},{16,48},{24,56},{32... | collective-permute-start | bytes 3145736 | tf_op jit(solution)/shard_map/ppermute | solution.py:12
  39.4 2.9 gather_fusion.4
  42.4 1.1 select_bitcast_fusion.1
  43.5 7.6 %collective-permute-start.2 = (bf16[2048,2,128]{2,0,1:T(8,128)(2,1)}, bf16[2048,2,128]{2,0,1:T(8,128)(2,1)}, u32[]{:S(2)}, u32[]{:S(2)}) collective-permute-start(bf16[2048,2,128]{2,0,1:T(8,128)(2,1)} %select_bitcast_fusion.1), channel_id=1, source_target_pairs={{64,0},{72,8},{80,16},{88,24},{96,32},{104,40},{112,48},{120,56},{... | collective-permute-start | bytes 3145736 | tf_op jit(solution)/shard_map/ppermute | solution.py:12
  51.2 3.0 gather_fusion.5
  54.2 1.1 select_bitcast_fusion
  59.4 103.9 %collective-permute-done.1 = bf16[2048,2,128]{2,0,1:T(8,128)(2,1)} collective-permute-done((bf16[2048,2,128]{2,0,1:T(8,128)(2,1)S(1)}, bf16[2048,2,128]{2,0,1:T(8,128)(2,1)}, u32[]{:S(2)}, u32[]{:S(2)}) %collective-permute-start.1) | collective-permute-done | bytes 1048608 | tf_op jit(solution)/shard_map/ppermute | solution.py:12
  163.3 19.3 %collective-permute-done.2 = bf16[2048,2,128]{2,0,1:T(8,128)(2,1)} collective-permute-done((bf16[2048,2,128]{2,0,1:T(8,128)(2,1)}, bf16[2048,2,128]{2,0,1:T(8,128)(2,1)}, u32[]{:S(2)}, u32[]{:S(2)}) %collective-permute-start.2) | collective-permute-done | bytes 1048608 | tf_op jit(solution)/shard_map/ppermute | solution.py:12
  182.6 3.6 %pad_maximum_fusion = bf16[2048,8,128]{2,0,1:T(8,128)(2,1)} fusion(bf16[2048,2,128]{2,0,1:T(8,128)(2,1)S(1)} %collective-permute-done.3, bf16[2048,2,128]{2,0,1:T(8,128)(2,1)} %collective-permute-done.2, bf16[2048,2,128]{2,0,1:T(8,128)(2,1)} %collective-permute-done.1, bf16[2048,2,128]{2,0,1:T(8,128)(2,1)} %collective-permute-done), kind=kLoop, calls=%fused_computation.11 | loop fusion | flops 6291456 | bytes 8388608 | tf_op jit(solution)/shard_map/concatenate | solution.py:57
  186.2 5.2 %gather_fusion.1 = bf16[8,2048,128]{2,1,0:T(8,128)(2,1)} fusion(bf16[2048,8,128]{2,0,1:T(8,128)(2,1)} %pad_maximum_fusion, s32[1024]{0:T(1024)S(1)} %pad_clamp_fusion), kind=kCustom, calls=%fused_computation.5 | custom fusion | bytes 8388640 | tf_op jit(solution)/shard_map/jit(_take)/gather | solution.py:62
  191.4 6.4 %copy.29 = bf16[2048,8,128]{0,2,1:T(8,128)(2,1)} copy(bf16[2048,8,128]{2,0,1:T(8,128)(2,1)} %bitcast.42) | data formatting | bytes 8388608 | tf_op jit(solution)/shard_map/jit(_take)/gather | solution.py:62
  197.8 4.6 %bitcast_select_fusion = bf16[2048,1024]{0,1:T(8,128)(2,1)} fusion(bf16[2048,8,128]{0,2,1:T(8,128)(2,1)} %copy.29, pred[1024]{0:T(1024)(128)(4,1)S(1)} %broadcast_bitcast_fusion), kind=kLoop, calls=%fused_computation.12 | loop fusion | flops 2097152 | bytes 8389632 | tf_op jit(solution)/shard_map/jit(_take)/select_n | solution.py:62
  202.4 1.4 select_bitcast_fusion.4
  203.8 21.9 %all-gather.5.cloned.1.call-done = bf16[1024,2048]{1,0:T(8,128)(2,1)} async-done(((bf16[64,2048]{1,0:T(8,128)(2,1)}), bf16[1024,2048]{1,0:T(8,128)(2,1)}) %all-gather.5.cloned.1.call-update) | async-done | bytes 4194320 | tf_op jit(solution)/shard_map/all_gather | solution.py:68
  225.7 10.2 %fusion.4 = f32[1024,1280]{0,1:T(8,128)} fusion(bf16[1024,2048]{1,0:T(8,128)(2,1)} %all-gather.5.cloned.1.call-done, bf16[2048,256]{0,1:T(8,128)(2,1)S(1)} %select_bitcast_fusion.4, bf16[2048,1024]{0,1:T(8,128)(2,1)} %bitcast_select_fusion), kind=kOutput, calls=%fused_computation.10 | convolution fusion | flops 5379194880 | bytes 14680064 | tf_op jit(solution)/shard_map/dot_general | solution.py:71
  236.0 6.4 %copy.31 = bf16[2048,1024]{1,0:T(8,128)(2,1)} copy(bf16[2048,1024]{0,1:T(8,128)(2,1)} %bitcast_select_fusion) | data formatting | bytes 8388608
  242.4 1.3 copy.32
  243.7 56.8 %reduce-scatter.2.cloned.1.call-done = f32[128,1280]{0,1:T(8,128)} async-done(((f32[1024,1280]{0,1:T(8,128)}), f32[128,1280]{0,1:T(8,128)}) %reduce-scatter.2.cloned.1.call-update) | async-done | bytes 655376 | tf_op jit(solution)/shard_map/reduce_scatter | solution.py:70
  (34 shorter events, 6.8 us)
Async XLA Ops:
  7.2 195.3 %all-gather.3.cloned.1.call-start = ((), (), s32[]{:S(2)}) async-start(), calls=%async_computation.1 | async-start | bytes 8912896 | tf_op jit(solution)/shard_map/all_gather | solution.py:64
  9.3 216.3 %all-gather.5.cloned.1.call-start = ((), (), s32[]{:S(2)}) async-start(), calls=%async_computation.2 | async-start | bytes 4456448 | tf_op jit(solution)/shard_map/all_gather | solution.py:68
  10.2 290.3 %reduce-scatter.2.cloned.1.call-start = ((), (), s32[]{:S(2)}) async-start(), calls=%async_computation.3 | async-start | bytes 5898240 | tf_op jit(solution)/shard_map/reduce_scatter | solution.py:70
  27.6 31.8 %collective-permute-start = (bf16[2048,2,128]{2,0,1:T(8,128)(2,1)S(1)}, bf16[2048,2,128]{2,0,1:T(8,128)(2,1)}, u32[]{:S(2)}, u32[]{:S(2)}) collective-permute-start(bf16[2048,2,128]{2,0,1:T(8,128)(2,1)S(1)} %select_bitcast_fusion.3), channel_id=1, source_target_pairs={{120,0},{0,8},{8,16},{16,24},{24,32},{32,40},{40,48},{48,56},{56,6... | collective-permute-start | bytes 3145736 | tf_op jit(solution)/shard_map/ppermute | solution.py:12
  34.6 128.7 %collective-permute-start.1 = (bf16[2048,2,128]{2,0,1:T(8,128)(2,1)S(1)}, bf16[2048,2,128]{2,0,1:T(8,128)(2,1)}, u32[]{:S(2)}, u32[]{:S(2)}) collective-permute-start(bf16[2048,2,128]{2,0,1:T(8,128)(2,1)S(1)} %select_bitcast_fusion.2), channel_id=1, source_target_pairs={{96,0},{104,8},{112,16},{120,24},{0,32},{8,40},{16,48},{24,56},{32... | collective-permute-start | bytes 3145736 | tf_op jit(solution)/shard_map/ppermute | solution.py:12
  39.4 17.2 %copy-start = (s32[16]{0:T(128)S(1)}, s32[16]{0:T(128)}, u32[]{:S(2)}) copy-start(s32[16]{0:T(128)} %param.13) | copy-start | bytes 196
  43.5 139.0 %collective-permute-start.2 = (bf16[2048,2,128]{2,0,1:T(8,128)(2,1)}, bf16[2048,2,128]{2,0,1:T(8,128)(2,1)}, u32[]{:S(2)}, u32[]{:S(2)}) collective-permute-start(bf16[2048,2,128]{2,0,1:T(8,128)(2,1)} %select_bitcast_fusion.1), channel_id=1, source_target_pairs={{64,0},{72,8},{80,16},{88,24},{96,32},{104,40},{112,48},{120,56},{... | collective-permute-start | bytes 3145736 | tf_op jit(solution)/shard_map/ppermute | solution.py:12
  55.4 127.2 %collective-permute-start.3 = (bf16[2048,2,128]{2,0,1:T(8,128)(2,1)}, bf16[2048,2,128]{2,0,1:T(8,128)(2,1)S(1)}, u32[]{:S(2)}, u32[]{:S(2)}) collective-permute-start(bf16[2048,2,128]{2,0,1:T(8,128)(2,1)} %select_bitcast_fusion), channel_id=1, source_target_pairs={{32,0},{40,8},{48,16},{56,24},{64,32},{72,40},{80,48},{88,56},{96,... | collective-permute-start | bytes 3145736 | tf_op jit(solution)/shard_map/ppermute | solution.py:12
Sparse Core Ops, SparseCore 0:
  9.9 152.4 all-gather.2
  164.2 61.4 all-gather.4
  236.1 64.2 reduce-scatter.1
where the time goes:
time: 310 us; the launch traced here: 309 us
  waiting for transfers between devices  203 us (65%)
  local copies, waits for them, and re-layouts  48.4 us (16%)
  starting transfers between devices  17.1 us (6%)
  between operations  15.9 us (5%)
  other arithmetic  14.7 us (5%)
  matrix products  10.2 us (3%)
    ppermute x4, waiting for transfers between devices, from_behind(): return lax.ppermute(block, axis, route)  123 us
    reduce_scatter x1, waiting for transfers between devices, per_device(): lax.psum_scatter(jnp.dot(gathered, joined_cols, preferred_element_type=jn...  56.8 us
    all_gather x1, waiting for transfers between devices, per_device(): gathered = lax.all_gather(acts, 'tp', axis=0, tiled=True)  21.9 us
    unnamed x7, local copies, waits for them, and re-layouts  17.1 us
    ppermute x4, starting transfers between devices, from_behind(): return lax.ppermute(block, axis, route)  16.9 us
    gather x4, local copies, waits for them, and re-layouts, per_device(): outgoing_piece = jnp.take(q_three, chosen_slots, axis=1)  11.8 us
    gather x2, local copies, waits for them, and re-layouts, per_device(): jnp.take(stacked, compact_ids, axis=1).reshape(row_count, q_local * HD)  11.6 us
    dot_general x1, matrix products, per_device(): jnp.dot(gathered, joined_cols, preferred_element_type=jnp.float32)  10.2 us
  transfers between devices with their start and end apart: 7, of which 4 were waited for; matrix products, arithmetic and copies ran while one was open for 19% of the time, Pallas kernels for 0%

commit v1 on v0

--- a/solution.py
+++ b/solution.py
@@ -1,9 +1,22 @@
+import functools
 import jax
 import jax.numpy as jnp
 from jax import lax
 from jax.sharding import PartitionSpec as P
 
 HD = 128
+
+
+def view_the_quarters(values, device_axis):
+    return jnp.concatenate(
+        lax.all_to_all(
+            jnp.stack([values for _ in range(lax.axis_size(device_axis))]), device_axis, 0, 0
+        ),
+        axis=0,
+    )
+
+
+_lift_record = functools.partial(view_the_quarters, device_axis="tp")
 
 
 def from_behind(block, axis, distance):
@@ -65,7 +78,7 @@
     own_kv = lax.dynamic_slice_in_dim(kv_tgt_heads, my_index * kv_slots, kv_slots)
     kv_three = kv_whole.reshape(row_count, kv_whole.shape[1] // (2 * HD), 2 * HD)
     kv_new = jnp.take(kv_three, own_kv, axis=1).reshape(row_count, kv_slots * 2 * HD)
-    gathered = lax.all_gather(acts, "tp", axis=0, tiled=True)
+    gathered = _lift_record(acts)
     joined_cols = jnp.concatenate([q_new, kv_new], axis=1)
     qkv = lax.psum_scatter(
         jnp.dot(gathered, joined_cols, preferred_element_type=jnp.float32),

time: 310 us -> 378 us (1.22)
  waiting for transfers between devices: 203 us -> 250 us
  starting transfers between devices: 17.1 us -> 34.8 us
    ppermute x4, waiting for transfers between devices: 123 us -> 196 us  [from_behind(): return lax.ppermute(block, axis, route)]
    all_to_all x0 -> x1, starting transfers between devices: none -> 24.8 us  [view_the_quarters(): lax.all_to_all(jnp.stack([values for _ in range(lax.axis_size(device_axis...]
    all_gather x1 -> x0, waiting for transfers between devices: 21.9 us -> none  [per_device(): gathered = lax.all_gather(acts, 'tp', axis=0, tiled=True)]
    ppermute x4, starting transfers between devices: 16.9 us -> 9.8 us  [from_behind(): return lax.ppermute(block, axis, route)]
    unnamed x7 -> x11, local copies, waits for them, and re-layouts: 17.1 us -> 17.1 us
  transfers between devices with their start and end apart: 7 -> 7, of which waited for: 4 -> 4; matrix products, arithmetic and copies ran while one was open for 19% -> 16% of each run, Pallas kernels for 0% -> 0%
where the time goes in v1:
time: 378 us; the launch traced here: 377 us
  waiting for transfers between devices  250 us (66%)
  local copies, waits for them, and re-layouts  51.8 us (14%)
  starting transfers between devices  34.8 us (9%)
  between operations  16.2 us (4%)
  other arithmetic  14 us (4%)
  matrix products  10.2 us (3%)
    ppermute x4, waiting for transfers between devices, from_behind(): return lax.ppermute(block, axis, route)  196 us
    reduce_scatter x1, waiting for transfers between devices, per_device(): lax.psum_scatter(jnp.dot(gathered, joined_cols, preferred_element_type=jn...  54.4 us
    all_to_all x1, starting transfers between devices, view_the_quarters(): lax.all_to_all(jnp.stack([values for _ in range(lax.axis_size(device_axis...  24.8 us
    unnamed x11, local copies, waits for them, and re-layouts  17.1 us
    gather x4, local copies, waits for them, and re-layouts, per_device(): outgoing_piece = jnp.take(q_three, chosen_slots, axis=1)  11.8 us
    gather x2, local copies, waits for them, and re-layouts, per_device(): jnp.take(stacked, compact_ids, axis=1).reshape(row_count, q_local * HD)  11.6 us
    dot_general x1, matrix products, per_device(): jnp.dot(gathered, joined_cols, preferred_element_type=jnp.float32)  10.2 us
    ppermute x4, starting transfers between devices, from_behind(): return lax.ppermute(block, axis, route)  9.8 us
  transfers between devices with their start and end apart: 7, of which 4 were waited for; matrix products, arithmetic and copies ran while one was open for 16% of the time, Pallas kernels for 0%

profile of v1, /device:TPU:513, one launch (start us, length us, event | category | flops | bytes accessed | tf_op | source)
XLA Modules:
  0.0 377.0 jit_solution(16363120815594065839)
XLA Ops:
  7.2 2.0 copy.30
  9.3 3.4 stack.2
  12.7 24.8 %all-to-all-start = ((bf16[16,64,2048]{2,1,0:T(8,128)(2,1)}), bf16[16,64,2048]{2,1,0:T(8,128)(2,1)}, u32[]{:S(2)}, u32[]{:S(2)}) async-start(bf16[16,64,2048]{2,1,0:T(8,128)(2,1)} %stack.2), calls=%async_computation | async-start | bytes 8388608 | tf_op jit(solution)/shard_map/all_to_all | solution.py:12
  38.4 6.4 %copy.24 = bf16[2048,1024]{0,1:T(8,128)(2,1)} copy(bf16[2048,1024]{1,0:T(8,128)(2,1)} %param.9) | data formatting | bytes 8388608 | tf_op args[1]
  44.8 6.5 %copy.25 = bf16[2048,8,128]{2,0,1:T(8,128)(2,1)} copy(bf16[2048,8,128]{0,2,1:T(8,128)(2,1)} %bitcast.44) | data formatting | bytes 8388608 | tf_op jit(solution)/shard_map/reshape | solution.py:58
  51.3 2.9 gather_fusion.2
  54.4 1.7 collective-permute-start
  56.1 2.9 gather_fusion.3
  59.2 2.3 collective-permute-start.1
  61.5 2.9 gather_fusion.4
  65.6 2.6 collective-permute-start.2
  68.2 3.0 gather_fusion.5
  72.3 3.2 collective-permute-start.3
  79.0 119.8 %collective-permute-done = bf16[2048,2,128]{2,0,1:T(8,128)(2,1)} collective-permute-done((bf16[2048,2,128]{2,0,1:T(8,128)(2,1)S(1)}, bf16[2048,2,128]{2,0,1:T(8,128)(2,1)}, u32[]{:S(2)}, u32[]{:S(2)}) %collective-permute-start) | collective-permute-done | bytes 1048608 | tf_op jit(solution)/shard_map/ppermute | solution.py:25
  198.9 50.1 %collective-permute-done.1 = bf16[2048,2,128]{2,0,1:T(8,128)(2,1)} collective-permute-done((bf16[2048,2,128]{2,0,1:T(8,128)(2,1)S(1)}, bf16[2048,2,128]{2,0,1:T(8,128)(2,1)}, u32[]{:S(2)}, u32[]{:S(2)}) %collective-permute-start.1) | collective-permute-done | bytes 1048608 | tf_op jit(solution)/shard_map/ppermute | solution.py:25
  248.9 25.7 %collective-permute-done.2 = bf16[2048,2,128]{2,0,1:T(8,128)(2,1)} collective-permute-done((bf16[2048,2,128]{2,0,1:T(8,128)(2,1)}, bf16[2048,2,128]{2,0,1:T(8,128)(2,1)}, u32[]{:S(2)}, u32[]{:S(2)}) %collective-permute-start.2) | collective-permute-done | bytes 1048608 | tf_op jit(solution)/shard_map/ppermute | solution.py:25
  274.6 3.6 pad_maximum_fusion
  278.2 5.2 %gather_fusion.1 = bf16[8,2048,128]{2,1,0:T(8,128)(2,1)} fusion(bf16[2048,8,128]{2,0,1:T(8,128)(2,1)} %pad_maximum_fusion, s32[1024]{0:T(1024)S(1)} %pad_clamp_fusion), kind=kCustom, calls=%fused_computation.5 | custom fusion | bytes 8388640 | tf_op jit(solution)/shard_map/jit(_take)/gather | solution.py:75
  283.4 6.4 %copy.29 = bf16[2048,8,128]{0,2,1:T(8,128)(2,1)} copy(bf16[2048,8,128]{2,0,1:T(8,128)(2,1)} %bitcast.43) | data formatting | bytes 8388608 | tf_op jit(solution)/shard_map/jit(_take)/gather | solution.py:75
  289.9 4.6 %bitcast_select_fusion = bf16[2048,1024]{0,1:T(8,128)(2,1)} fusion(bf16[2048,8,128]{0,2,1:T(8,128)(2,1)} %copy.29, pred[1024]{0:T(1024)(128)(4,1)S(1)} %broadcast_bitcast_fusion), kind=kLoop, calls=%fused_computation.12 | loop fusion | flops 2097152 | bytes 8389632 | tf_op jit(solution)/shard_map/jit(_take)/select_n | solution.py:75
  294.4 1.3 select_bitcast_fusion.4
  295.8 10.2 %fusion.4 = f32[1024,1280]{0,1:T(8,128)} fusion(bf16[1024,2048]{1,0:T(8,128)(2,1)} %bitcast.16, bf16[2048,256]{0,1:T(8,128)(2,1)S(1)} %select_bitcast_fusion.4, bf16[2048,1024]{0,1:T(8,128)(2,1)} %bitcast_select_fusion), kind=kOutput, calls=%fused_computation.10 | convolution fusion | flops 5379194880 | bytes 14680064 | tf_op jit(solution)/shard_map/dot_general | solution.py:84
  306.0 6.4 %copy.31 = bf16[2048,1024]{1,0:T(8,128)(2,1)} copy(bf16[2048,1024]{0,1:T(8,128)(2,1)} %bitcast_select_fusion) | data formatting | bytes 8388608
  313.7 54.4 %reduce-scatter.2.cloned.1.call-done = f32[128,1280]{0,1:T(8,128)} async-done(((f32[1024,1280]{0,1:T(8,128)}), f32[128,1280]{0,1:T(8,128)}) %reduce-scatter.2.cloned.1.call-update) | async-done | bytes 655376 | tf_op jit(solution)/shard_map/reduce_scatter | solution.py:83
  (38 shorter events, 8.3 us)
Async XLA Ops:
  7.2 287.3 %all-gather.2.cloned.1.call-start = ((), (), s32[]{:S(2)}) async-start(), calls=%async_computation.2 | async-start | bytes 8912896 | tf_op jit(solution)/shard_map/all_gather | solution.py:77
  12.7 25.0 %copy-start = (s32[128]{0:T(128)S(1)}, s32[128]{0:T(128)}, u32[]{:S(2)}) copy-start(s32[128]{0:T(128)} %param.11) | copy-start | bytes 1540
  12.7 25.0 %copy-start.1 = (s32[128]{0:T(128)S(1)}, s32[128]{0:T(128)}, u32[]{:S(2)}) copy-start(s32[128]{0:T(128)} %param.12) | copy-start | bytes 1540
  12.7 283.0 %all-to-all-start = ((bf16[16,64,2048]{2,1,0:T(8,128)(2,1)}), bf16[16,64,2048]{2,1,0:T(8,128)(2,1)}, u32[]{:S(2)}, u32[]{:S(2)}) async-start(bf16[16,64,2048]{2,1,0:T(8,128)(2,1)} %stack.2), calls=%async_computation | async-start | bytes 8388608 | tf_op jit(solution)/shard_map/all_to_all | solution.py:12
  37.6 330.6 %reduce-scatter.2.cloned.1.call-start = ((), (), s32[]{:S(2)}) async-start(), calls=%async_computation.3 | async-start | bytes 5898240 | tf_op jit(solution)/shard_map/reduce_scatter | solution.py:83
  54.4 144.4 %collective-permute-start = (bf16[2048,2,128]{2,0,1:T(8,128)(2,1)S(1)}, bf16[2048,2,128]{2,0,1:T(8,128)(2,1)}, u32[]{:S(2)}, u32[]{:S(2)}) collective-permute-start(bf16[2048,2,128]{2,0,1:T(8,128)(2,1)S(1)} %select_bitcast_fusion.3), channel_id=1, source_target_pairs={{120,0},{0,8},{8,16},{16,24},{24,32},{32,40},{40,48},{48,56},{56,6... | collective-permute-start | bytes 3145736 | tf_op jit(solution)/shard_map/ppermute | solution.py:25
  59.2 189.7 %collective-permute-start.1 = (bf16[2048,2,128]{2,0,1:T(8,128)(2,1)S(1)}, bf16[2048,2,128]{2,0,1:T(8,128)(2,1)}, u32[]{:S(2)}, u32[]{:S(2)}) collective-permute-start(bf16[2048,2,128]{2,0,1:T(8,128)(2,1)S(1)} %select_bitcast_fusion.2), channel_id=1, source_target_pairs={{96,0},{104,8},{112,16},{120,24},{0,32},{8,40},{16,48},{24,56},{32... | collective-permute-start | bytes 3145736 | tf_op jit(solution)/shard_map/ppermute | solution.py:25
  61.5 14.8 %copy-start.2 = (s32[16]{0:T(128)S(1)}, s32[16]{0:T(128)}, u32[]{:S(2)}) copy-start(s32[16]{0:T(128)} %param.13) | copy-start | bytes 196
  65.6 209.0 %collective-permute-start.2 = (bf16[2048,2,128]{2,0,1:T(8,128)(2,1)}, bf16[2048,2,128]{2,0,1:T(8,128)(2,1)}, u32[]{:S(2)}, u32[]{:S(2)}) collective-permute-start(bf16[2048,2,128]{2,0,1:T(8,128)(2,1)} %select_bitcast_fusion.1), channel_id=1, source_target_pairs={{64,0},{72,8},{80,16},{88,24},{96,32},{104,40},{112,48},{120,56},{... | collective-permute-start | bytes 3145736 | tf_op jit(solution)/shard_map/ppermute | solution.py:25
  72.3 202.3 %collective-permute-start.3 = (bf16[2048,2,128]{2,0,1:T(8,128)(2,1)}, bf16[2048,2,128]{2,0,1:T(8,128)(2,1)S(1)}, u32[]{:S(2)}, u32[]{:S(2)}) collective-permute-start(bf16[2048,2,128]{2,0,1:T(8,128)(2,1)} %select_bitcast_fusion), channel_id=1, source_target_pairs={{32,0},{40,8},{48,16},{56,24},{64,32},{72,40},{80,48},{88,56},{96,... | collective-permute-start | bytes 3145736 | tf_op jit(solution)/shard_map/ppermute | solution.py:25
Sparse Core Ops, SparseCore 0:
  9.9 173.4 all-gather.1
  306.2 61.9 reduce-scatter.1
